TPU v7x, 128 devices: a whole 4x4x4 slice. The times are simulated.
128 devices in a mesh: ctx: 16 (over z, x), bulk: 8 (over y, core).
Axes of the slice: x: 4, y: 4, z: 4, core: 2. Of those that a mesh axis runs over, the one named last changes fastest.
Arguments:
- query: bfloat16 [32768, 5120], P(('ctx', 'bulk')), may hold values from -1 to 1
- keys: bfloat16 [32768, 1024], P(('ctx', 'bulk')), may hold values from -1 to 1
- values: bfloat16 [32768, 1024], P(('ctx', 'bulk')), may hold values from -6 to 6
- output: bfloat16 [32768, 5120], P(('ctx', 'bulk')), may hold values from -3 to 3
- grad_out: bfloat16 [32768, 5120], P(('ctx', 'bulk')), may hold values from -12 to 12
- logsumexp: float32 [32768, 40], P(('ctx', 'bulk')), may hold values from 3 to 5
- selected: int32 [256, 8, 3], P(('ctx', 'bulk')), may hold values from -1 to 255, as said below
Outputs:
- grad_query: bfloat16 [32768, 5120], P(('ctx', 'bulk'))
- grad_keys: bfloat16 [32768, 1024], P(('ctx', 'bulk'))
- grad_values: bfloat16 [32768, 1024], P(('ctx', 'bulk'))
Inputs may be any that keep to these rules, and one draw needn't show every extreme that they name: `selected`: entry [b, h, s] is -1 (no block) or a block on a device before the device of block b. Over all entries of one device's 2 blocks, each other device is named at most once; a device with 48 or more devices before it has no -1. Every device but the first names the device just before it, and the last device names the first device.
All inputs are finite; a program needn't handle non-finite values.
Results may differ from a plain program's by a relative error of at most 0.0062.
Values may be sent and summed in bfloat16 or wider, within the bound.
A program may use at most 192 MiB of HBM per device.

v0:
```python
import jax
import jax.numpy as jnp
from jax import lax
from jax.sharding import PartitionSpec as P

HD = 128
KVH = 8
GROUP = 5
BLK = 128
TOPK = 3


def block_grads(item):
    queries, grads, stats, shifts, key_sets, usable = item
    scale = HD ** (-0.5)
    key_set = key_sets[..., :HD]
    value_set = key_sets[..., HD:]
    length = queries.shape[0]
    positions = jnp.arange(length, dtype=jnp.int32)
    causal = positions[None, :] <= positions[:, None]
    slot_ids = jnp.arange(key_sets.shape[1], dtype=jnp.int32)
    allowed = (slot_ids[None, :, None] > 0) | causal[:, None, :]
    mask = usable[:, None, None, :, None] & allowed[None, None]
    scores = (
        jnp.einsum("qhgd,hjkd->hgqjk", queries, key_set, preferred_element_type=jnp.float32) * scale
    )
    logs = jnp.transpose(stats, (1, 2, 0))[..., None, None]
    probs32 = jnp.where(mask, jnp.exp(scores - logs), 0.0)
    probs = probs32.astype(jnp.bfloat16)
    value_part = jnp.einsum("hgqjk,qhgd->hjkd", probs, grads, preferred_element_type=jnp.float32)
    dprobs = jnp.einsum("qhgd,hjkd->hgqjk", grads, value_set, preferred_element_type=jnp.float32)
    offsets = jnp.transpose(shifts, (1, 2, 0))[..., None, None]
    dscores = (probs32 * (dprobs - offsets)).astype(jnp.bfloat16)
    query_grad = (
        jnp.einsum("hgqjk,hjkd->qhgd", dscores, key_set, preferred_element_type=jnp.float32) * scale
    )
    key_part = (
        jnp.einsum("hgqjk,qhgd->hjkd", dscores, queries, preferred_element_type=jnp.float32) * scale
    )
    flat_grad = query_grad.astype(jnp.bfloat16).reshape(length, -1)
    return (flat_grad, jnp.concatenate([key_part, value_part], axis=-1))


def shards(query, keys, values, output, grad_out, logsumexp, selected):
    count_peers = lax.axis_size(("ctx", "bulk"))
    tok_rows = query.shape[0]
    local_blocks = tok_rows // BLK
    per_device = local_blocks * KVH * TOPK
    key_rows = keys.reshape(local_blocks, BLK, KVH, HD)
    value_rows = values.reshape(local_blocks, BLK, KVH, HD)
    kv_table = jnp.transpose(jnp.concatenate([key_rows, value_rows], axis=3), (0, 2, 1, 3))
    kv_flat = kv_table.reshape(local_blocks * KVH, BLK, 2 * HD)
    chosen = selected.reshape(per_device)
    owners = jnp.where(chosen >= 0, chosen // local_blocks, -1)
    head_of = jnp.arange(per_device, dtype=jnp.int32) // TOPK % KVH
    item_code = chosen % local_blocks * KVH + head_of
    peer_ids = jnp.arange(count_peers, dtype=jnp.int32)
    matches = owners[:, None] == peer_ids[None, :]
    request = jnp.max(jnp.where(matches, item_code[:, None], -1), axis=0)
    incoming = lax.all_to_all(
        request.reshape(count_peers, 1), ("ctx", "bulk"), split_axis=0, concat_axis=0, tiled=True
    ).reshape(count_peers)
    outgoing = jnp.take(kv_flat, jnp.maximum(incoming, 0), axis=0)
    outgoing = jnp.where((incoming >= 0)[:, None, None], outgoing, jnp.zeros_like(outgoing))
    arrived = lax.all_to_all(outgoing, ("ctx", "bulk"), split_axis=0, concat_axis=0, tiled=True)
    fetched = jnp.take(arrived, jnp.maximum(owners, 0), axis=0).reshape(
        local_blocks, KVH, TOPK, BLK, 2 * HD
    )
    key_sets = jnp.concatenate([kv_table[:, :, None], fetched], axis=2)
    usable = jnp.concatenate(
        [
            jnp.ones((local_blocks, KVH, 1), jnp.bool_),
            (chosen >= 0).reshape(local_blocks, KVH, TOPK),
        ],
        axis=2,
    )
    query_blocks = query.reshape(local_blocks, BLK, KVH, GROUP, HD)
    grad_blocks = grad_out.reshape(local_blocks, BLK, KVH, GROUP, HD)
    shifts = jnp.sum(
        grad_out.astype(jnp.float32).reshape(tok_rows, KVH, GROUP, HD)
        * output.astype(jnp.float32).reshape(tok_rows, KVH, GROUP, HD),
        axis=-1,
    )
    shifts = shifts.reshape(local_blocks, BLK, KVH, GROUP)
    stats = logsumexp.reshape(local_blocks, BLK, KVH, GROUP)
    query_grads, partials = lax.map(
        block_grads, (query_blocks, grad_blocks, stats, shifts, key_sets, usable)
    )
    own_part = partials[:, :, 0].reshape(local_blocks * KVH, BLK * 2 * HD)
    remote = partials[:, :, 1:].reshape(per_device, BLK * 2 * HD)
    target = jnp.where(owners >= 0, owners, count_peers)
    returning = (
        jnp.zeros((count_peers, BLK * 2 * HD), jnp.float32).at[target].set(remote, mode="drop")
    )
    returning = returning.reshape(count_peers, BLK, 2 * HD)
    received = lax.all_to_all(
        returning.astype(jnp.bfloat16), ("ctx", "bulk"), split_axis=0, concat_axis=0, tiled=True
    ).astype(returning.dtype)
    received_flat = received.reshape(count_peers, BLK * 2 * HD)
    received_flat = jnp.where((incoming >= 0)[:, None], received_flat, 0.0)
    total = own_part.at[jnp.maximum(incoming, 0)].add(received_flat)
    total = jnp.transpose(total.reshape(local_blocks, KVH, BLK, 2 * HD), (0, 2, 1, 3))
    grad_query = query_grads.reshape(tok_rows, KVH * GROUP * HD)
    grad_keys = total[..., :HD].reshape(tok_rows, KVH * HD).astype(jnp.bfloat16)
    grad_values = total[..., HD:].reshape(tok_rows, KVH * HD).astype(jnp.bfloat16)
    return (grad_query, grad_keys, grad_values)


def solution(mesh):
    in_specs = (
        P(("ctx", "bulk"), None),
        P(("ctx", "bulk"), None),
        P(("ctx", "bulk"), None),
        P(("ctx", "bulk"), None),
        P(("ctx", "bulk"), None),
        P(("ctx", "bulk"), None),
        P(("ctx", "bulk"), None, None),
    )
    out_specs = (P(("ctx", "bulk"), None), P(("ctx", "bulk"), None), P(("ctx", "bulk"), None))
    return jax.shard_map(shards, mesh=mesh, in_specs=in_specs, out_specs=out_specs, check_vma=False)
```

profile of v0, /device:TPU:15, one launch (start us, length us, event | category | flops | bytes accessed | tf_op | source)
XLA Modules:
  0.0 434.6 jit_solution(18173230589886575037)
XLA Ops:
  2.4 10.6 %all-to-all-start = ((s32[128,1,1]{2,1,0:T(1,128)}), s32[128,1,1]{2,1,0:T(1,128)S(1)}, u32[]{:S(2)}, u32[]{:S(2)}) async-start(s32[128,1,1]{2,1,0:T(1,128)} %copy.155), calls=%async_computation | async-start | bytes 131072 | tf_op jit(solution)/shard_map/all_to_all | solution.py:60
  16.8 3.3 all-to-all-done
  22.5 6.5 %gather_fusion = bf16[128,128,256]{2,1,0:T(8,128)(2,1)} fusion(bf16[16,128,256]{2,1,0:T(8,128)(2,1)S(1)} %bitcast.192, s32[1024]{0:T(1024)S(1)} %pad_clamp_fusion.1), kind=kCustom, calls=%fused_computation | custom fusion | bytes 16777728 | tf_op jit(solution)/shard_map/jit(_take)/gather | solution.py:63
  28.9 4.6 %compare_reduce_fusion.1 = (pred[128]{0:T(512)(128)(4,1)S(1)}, pred[128]{0:T(512)(128)(4,1)S(1)}) fusion(s32[128,1,1]{2,1,0:T(1,128)S(1)} %all-to-all-done), kind=kLoop, calls=%fused_computation.63 | loop fusion | flops 384 | bytes 768 | tf_op jit(solution)/shard_map/ge | solution.py:64
  34.1 7.5 %select_select_fusion = bf16[128,128,256]{2,1,0:T(8,128)(2,1)} fusion(bf16[128,128,256]{2,1,0:T(8,128)(2,1)} %gather_fusion, pred[128]{0:T(512)(128)(4,1)S(1)} %get-tuple-element.99, pred[128]{0:T(512)(128)(4,1)S(1)} %get-tuple-element.98), kind=kLoop, calls=%fused_computation.54 | loop fusion | flops 8388608 | bytes 16777472 | tf_op jit(solution)/shard_map/jit(_where)/select_n | solution.py:64
  41.6 8.7 %all-to-all-start.1 = ((bf16[128,128,256]{2,1,0:T(8,128)(2,1)}), bf16[128,128,256]{2,1,0:T(8,128)(2,1)}, u32[]{:S(2)}, u32[]{:S(2)}) async-start(bf16[128,128,256]{2,1,0:T(8,128)(2,1)} %select_select_fusion), calls=%async_computation.1 | async-start | bytes 16777216 | tf_op jit(solution)/shard_map/all_to_all | solution.py:65
  50.4 4.4 %reshape.364 = bf16[2,128,8,5,128]{4,3,2,1,0:T(8,128)(2,1)} reshape(bf16[256,5120]{1,0:T(8,128)(2,1)S(1)} %copy-done.5) | data formatting | bytes 5242880 | tf_op jit(solution)/shard_map/reshape | solution.py:78
  60.4 7.1 %reshape.363 = bf16[2,128,8,5,128]{4,3,2,1,0:T(8,128)(2,1)} reshape(bf16[256,5120]{1,0:T(8,128)(2,1)} %param.9) | data formatting | bytes 5242880 | tf_op jit(solution)/shard_map/reshape | solution.py:77
  67.5 5.7 %copy.164 = bf16[2,128,8,5,128]{4,1,3,2,0:T(8,128)(2,1)} copy(bf16[2,128,8,5,128]{4,3,2,1,0:T(8,128)(2,1)} %reshape.363) | data formatting | bytes 5242880 | tf_op jit(solution)/shard_map/while | solution.py:86
  73.2 5.6 %copy.166 = bf16[2,128,8,5,128]{4,1,3,2,0:T(8,128)(2,1)} copy(bf16[2,128,8,5,128]{4,3,2,1,0:T(8,128)(2,1)} %reshape.364) | data formatting | bytes 5242880 | tf_op jit(solution)/shard_map/while | solution.py:86
  78.8 4.4 %copy.162 = bf16[256,5120]{0,1:T(8,128)(2,1)} copy(bf16[256,5120]{1,0:T(8,128)(2,1)} %param.12) | data formatting | bytes 5242880 | tf_op args[3]
  83.2 4.7 %convert_multiply_fusion = f32[256,5120]{0,1:T(8,128)} fusion(bf16[256,5120]{0,1:T(8,128)(2,1)} %copy.162, bf16[256,5120]{0,1:T(8,128)(2,1)S(1)} %copy.161), kind=kLoop, calls=%fused_computation.55 | loop fusion | flops 3932160 | bytes 10485760 | tf_op jit(solution)/shard_map/mul | solution.py:80
  91.4 58.6 %all-to-all-done.1 = bf16[128,128,256]{2,1,0:T(8,128)(2,1)} async-done(((bf16[128,128,256]{2,1,0:T(8,128)(2,1)}), bf16[128,128,256]{2,1,0:T(8,128)(2,1)}, u32[]{:S(2)}, u32[]{:S(2)}) %all-to-all-start.1) | async-done | bytes 8388640 | tf_op jit(solution)/shard_map/all_to_all | solution.py:65
  150.0 4.1 gather_fusion.1
  157.7 62.1 %while.12 = (s32[]{:T(128)}, bf16[2,128,5120]{2,1,0:T(8,128)(2,1)}, f32[2,8,4,128,256]{3,4,2,1,0:T(8,128)}, bf16[2,8,4,128,256]{4,3,2,1,0:T(8,128)(2,1)}, pred[2...) while((s32[]{:T(128)}, bf16[2,128,5120]{2,1,0:T(8,128)(2,1)}, ...), condition=%wide.region_3.4_spmd, body=%wide.region_2.3_spmd.sunk | while | flops 3385147392 | bytes 142758400 | solution.py:86
  160.4 5.5 %fusion.67 = f32[8,4,128,128,5]{3,2,4,1,0:T(8,128)} fusion(bf16[2,128,8,5,128]{4,1,3,2,0:T(8,128)(2,1)S(1)} %copy-done.1, s32[]{:T(128)S(6)} %copy.248, bf16[8,4,128,256]{3,2,1,0:T(8,128)(2,1)S(1)} %dynamic-slice_bitcast_fusion.2), kind=kOutput, calls=%fused_computation.26.clone.1 | convolution fusion | flops 671088640 | bytes 12845060 | tf_op jit(solution)/shard_map/while/body/eval_jaxpr/qhgd,hjkd->hgqjk/dot_general | solution.py:25
  166.6 6.5 %fusion.69 = bf16[8,5,128,4,128]{2,4,1,3,0:T(8,128)(2,1)S(1)} fusion(f32[8,4,128,128,5]{3,2,4,1,0:T(8,128)} %fusion.67, f32[8,5,128]{2,1,0:T(8,128)S(1)} %bitcast.209, f32[8,5,128]{2,1,0:T(8,128)S(1)} %bitcast.207, pred[8,128,4,128]{1,3,2,0:T(8,128)(4,1)S(1)} %broadcast_and_fusion.2, bf16[2,128,8,5,128]{4,1,3,2,0:T(8,128)(2,1)} %get-tuple-element.216, ...), kind=kOutput, calls=%fused_computation.6.clone.1 | convolution fusion | flops 686817280 | bytes 18677764 | tf_op jit(solution)/shard_map/while/body/eval_jaxpr/qhgd,hjkd->hgqjk/dot_general | solution.py:31
  178.3 6.4 %fusion.71 = f32[8,4,128,128]{2,3,1,0:T(8,128)S(1)} fusion(f32[8,4,128,128,5]{3,2,4,1,0:T(8,128)} %fusion.67, f32[8,5,128]{2,1,0:T(8,128)S(1)} %bitcast.208, pred[8,128,4,128]{1,3,2,0:T(8,128)(4,1)S(1)} %copy-done.4, bf16[2,128,8,5,128]{4,1,3,2,0:T(8,128)(2,1)} %get-tuple-element.216, s32[]{:T(128)S(6)} %copy.248), kind=kOutput, calls=%fused_computation.22.clone.1 | convolution fusion | flops 681574400 | bytes 14438404 | tf_op jit(solution)/shard_map/while/body/eval_jaxpr/hgqjk,qhgd->hjkd/dot_general | solution.py:30
  191.3 5.5 %fusion.67 = f32[8,4,128,128,5]{3,2,4,1,0:T(8,128)} fusion(bf16[2,128,8,5,128]{4,1,3,2,0:T(8,128)(2,1)S(1)} %copy-done.1, s32[]{:T(128)S(6)} %copy.248, bf16[8,4,128,256]{3,2,1,0:T(8,128)(2,1)S(1)} %dynamic-slice_bitcast_fusion.2), kind=kOutput, calls=%fused_computation.26.clone.1 | convolution fusion | flops 671088640 | bytes 12845060 | tf_op jit(solution)/shard_map/while/body/eval_jaxpr/qhgd,hjkd->hgqjk/dot_general | solution.py:25
  197.4 6.5 %fusion.69 = bf16[8,5,128,4,128]{2,4,1,3,0:T(8,128)(2,1)S(1)} fusion(f32[8,4,128,128,5]{3,2,4,1,0:T(8,128)} %fusion.67, f32[8,5,128]{2,1,0:T(8,128)S(1)} %bitcast.209, f32[8,5,128]{2,1,0:T(8,128)S(1)} %bitcast.207, pred[8,128,4,128]{1,3,2,0:T(8,128)(4,1)S(1)} %broadcast_and_fusion.2, bf16[2,128,8,5,128]{4,1,3,2,0:T(8,128)(2,1)} %get-tuple-element.216, ...), kind=kOutput, calls=%fused_computation.6.clone.1 | convolution fusion | flops 686817280 | bytes 18677764 | tf_op jit(solution)/shard_map/while/body/eval_jaxpr/qhgd,hjkd->hgqjk/dot_general | solution.py:31
  209.2 6.4 %fusion.71 = f32[8,4,128,128]{2,3,1,0:T(8,128)S(1)} fusion(f32[8,4,128,128,5]{3,2,4,1,0:T(8,128)} %fusion.67, f32[8,5,128]{2,1,0:T(8,128)S(1)} %bitcast.208, pred[8,128,4,128]{1,3,2,0:T(8,128)(4,1)S(1)} %copy-done.4, bf16[2,128,8,5,128]{4,1,3,2,0:T(8,128)(2,1)} %get-tuple-element.216, s32[]{:T(128)S(6)} %copy.248), kind=kOutput, calls=%fused_computation.22.clone.1 | convolution fusion | flops 681574400 | bytes 14438404 | tf_op jit(solution)/shard_map/while/body/eval_jaxpr/hgqjk,qhgd->hjkd/dot_general | solution.py:30
  219.8 6.1 %slice.21 = f32[2,8,3,128,256]{3,4,2,1,0:T(8,128)} slice(f32[2,8,4,128,256]{3,4,2,1,0:T(8,128)} %get-tuple-element.52), slice={[0:2], [0:8], [1:4], [0:128], [0:256]} | slice | bytes 12582912 | tf_op jit(solution)/shard_map/slice | solution.py:90
  225.9 6.7 %copy.170 = f32[2,8,3,128,256]{4,3,2,1,0:T(8,128)} copy(f32[2,8,3,128,256]{3,4,2,1,0:T(8,128)} %slice.21) | data formatting | bytes 12582912 | tf_op jit(solution)/shard_map/slice | solution.py:90
  232.7 9.1 %copy.204 = f32[6,8,128,256]{3,1,2,0:T(8,128)} copy(f32[6,8,128,256]{3,2,1,0:T(8,128)} %bitcast.196) | data formatting | bytes 12582912
  241.7 12.9 %scatter_custom_fusion = f32[128,32768]{1,0:T(8,128)} fusion(s32[48]{0:T(128)} %get-tuple-element.118, f32[48,32768]{1,0:T(8,128)} %bitcast.201, f32[]{:T(128)} %constant.107.clone.1), kind=kCustom, calls=%fused_computation.52 | custom fusion | bytes 16777728 | tf_op jit(solution)/shard_map/scatter | solution.py:93
  254.6 8.8 %convert_element_type.35 = bf16[128,32768]{1,0:T(8,128)(2,1)} convert(f32[128,32768]{1,0:T(8,128)} %scatter_custom_fusion) | non-fusion elementwise | flops 4194304 | bytes 25165824 | tf_op jit(solution)/shard_map/convert_element_type | solution.py:97
  263.4 9.1 %copy.205 = bf16[16,8,128,256]{3,2,1,0:T(8,128)(2,1)} copy(bf16[16,8,128,256]{3,1,2,0:T(8,128)(2,1)} %bitcast.194) | data formatting | bytes 16777216
  272.5 8.2 %all-to-all-start.2 = ((bf16[128,128,256]{2,1,0:T(8,128)(2,1)}), bf16[128,128,256]{2,1,0:T(8,128)(2,1)}, u32[]{:S(2)}, u32[]{:S(2)}) async-start(bf16[128,128,256]{2,1,0:T(8,128)(2,1)} %bitcast.195), calls=%async_computation.2 | async-start | bytes 16777216 | tf_op jit(solution)/shard_map/all_to_all | solution.py:96
  286.1 94.9 %all-to-all-done.2 = bf16[128,128,256]{2,1,0:T(8,128)(2,1)} async-done(((bf16[128,128,256]{2,1,0:T(8,128)(2,1)}), bf16[128,128,256]{2,1,0:T(8,128)(2,1)}, u32[]{:S(2)}, u32[]{:S(2)}) %all-to-all-start.2) | async-done | bytes 8388640 | tf_op jit(solution)/shard_map/all_to_all | solution.py:96
  381.0 16.0 %copy.206 = f32[16,8,128,256]{3,1,2,0:T(8,128)} copy(bf16[16,8,128,256]{3,2,1,0:T(8,128)(2,1)} %bitcast.136) | data formatting | bytes 25165824
  397.1 11.4 %broadcast_select_fusion = f32[128,32768]{1,0:T(8,128)} fusion(f32[128,32768]{1,0:T(8,128)} %bitcast.193, pred[128]{0:T(512)(128)(4,1)S(1)} %copy-done.11), kind=kLoop, calls=%fused_computation.51 | loop fusion | flops 4194304 | bytes 33554560 | tf_op jit(solution)/shard_map/jit(_where)/select_n | solution.py:100
  408.5 24.5 %scatter_fusion = f32[16,32768]{1,0:T(8,128)S(1)} fusion(f32[16,32768]{1,0:T(8,128)S(1)} %bitcast.188, s32[128]{0:T(128)S(1)} %copy-done.13, f32[128,32768]{1,0:T(8,128)} %broadcast_select_fusion), kind=kCustom, calls=%fused_computation.3 | custom fusion | flops 4194304 | bytes 50332160 | tf_op jit(solution)/shard_map/scatter-add | solution.py:101
  (111 shorter events, 52.5 us)
Async XLA Ops:
  2.4 17.7 %all-to-all-start = ((s32[128,1,1]{2,1,0:T(1,128)}), s32[128,1,1]{2,1,0:T(1,128)S(1)}, u32[]{:S(2)}, u32[]{:S(2)}) async-start(s32[128,1,1]{2,1,0:T(1,128)} %copy.155), calls=%async_computation | async-start | bytes 131072 | tf_op jit(solution)/shard_map/all_to_all | solution.py:60
  15.5 1.1 copy-start.6
  22.5 6.5 %copy-start.12 = (s32[128]{0:T(128)}, s32[128]{0:T(128)S(1)}, u32[]{:S(2)}) copy-start(s32[128]{0:T(128)S(1)} %maximum_reduce_fusion) | copy-start | bytes 1540
  33.6 0.5 copy-start.10
  41.6 8.8 %copy-start.5 = (bf16[256,5120]{1,0:T(8,128)(2,1)S(1)}, bf16[256,5120]{1,0:T(8,128)(2,1)}, u32[]{:S(2)}) copy-start(bf16[256,5120]{1,0:T(8,128)(2,1)} %param.13) | copy-start | bytes 7864324
  41.6 108.4 %all-to-all-start.1 = ((bf16[128,128,256]{2,1,0:T(8,128)(2,1)}), bf16[128,128,256]{2,1,0:T(8,128)(2,1)}, u32[]{:S(2)}, u32[]{:S(2)}) async-start(bf16[128,128,256]{2,1,0:T(8,128)(2,1)} %select_select_fusion), calls=%async_computation.1 | async-start | bytes 16777216 | tf_op jit(solution)/shard_map/all_to_all | solution.py:65
  54.8 3.0 copy-start.9
  67.5 5.7 %copy-start.8 = (f32[256,40]{0,1:T(8,128)S(1)}, f32[256,40]{0,1:T(8,128)}, u32[]{:S(2)}) copy-start(f32[256,40]{0,1:T(8,128)} %param.14) | copy-start | bytes 122884
  154.1 1.2 copy-start.7
  158.1 2.4 copy-start.1
  166.6 6.5 %copy-start.3 = (pred[8,128,4,128]{1,3,2,0:T(8,128)(4,1)}, pred[8,128,4,128]{1,3,2,0:T(8,128)(4,1)S(1)}, u32[]{:S(2)}) copy-start(pred[8,128,4,128]{1,3,2,0:T(8,128)(4,1)S(1)} %broadcast_and_fusion.2) | copy-start | bytes 1572868 | tf_op jit(solution)/shard_map/while
  173.1 2.4 copy-start
  176.5 1.8 copy-start.4
  177.2 7.5 %slice-start = ((s8[5242880]{0:T(1024)(128)(4,1)}), s8[4194304]{0:T(1024)(128)(4,1)S(1)}, s32[]{:S(2)}) async-start(s8[5242880]{0:T(1024)(128)(4,1)} %bitcast.189), calls=%async_computation.3 | async-start | bytes 8388608 | tf_op jit(solution)/shard_map/while
  178.3 6.4 %slice-start.1 = ((s8[5242880]{0:T(1024)(128)(4,1)}), s8[1048576]{0:T(1024)(128)(4,1)S(1)}, s32[]{:S(2)}) async-start(s8[5242880]{0:T(1024)(128)(4,1)} %bitcast.189), calls=%async_computation.4 | async-start | bytes 2097152 | tf_op jit(solution)/shard_map/while
  178.3 6.4 %copy-start.2 = (bf16[2,128,8,5,128]{4,1,3,2,0:T(8,128)(2,1)S(1)}, bf16[2,128,8,5,128]{4,1,3,2,0:T(8,128)(2,1)}, u32[]{:S(2)}) copy-start(bf16[2,128,8,5,128]{4,1,3,2,0:T(8,128)(2,1)} %get-tuple-element.214) | copy-start | bytes 7864324 | tf_op jit(solution)/shard_map/while
  188.9 2.4 copy-start.1
  197.4 6.5 %copy-start.3 = (pred[8,128,4,128]{1,3,2,0:T(8,128)(4,1)}, pred[8,128,4,128]{1,3,2,0:T(8,128)(4,1)S(1)}, u32[]{:S(2)}) copy-start(pred[8,128,4,128]{1,3,2,0:T(8,128)(4,1)S(1)} %broadcast_and_fusion.2) | copy-start | bytes 1572868 | tf_op jit(solution)/shard_map/while
  203.9 2.4 copy-start
  207.4 1.8 copy-start.4
  208.0 7.5 %slice-start = ((s8[5242880]{0:T(1024)(128)(4,1)}), s8[4194304]{0:T(1024)(128)(4,1)S(1)}, s32[]{:S(2)}) async-start(s8[5242880]{0:T(1024)(128)(4,1)} %bitcast.189), calls=%async_computation.3 | async-start | bytes 8388608 | tf_op jit(solution)/shard_map/while
  209.2 6.4 %slice-start.1 = ((s8[5242880]{0:T(1024)(128)(4,1)}), s8[1048576]{0:T(1024)(128)(4,1)S(1)}, s32[]{:S(2)}) async-start(s8[5242880]{0:T(1024)(128)(4,1)} %bitcast.189), calls=%async_computation.4 | async-start | bytes 2097152 | tf_op jit(solution)/shard_map/while
  209.2 6.4 %copy-start.2 = (bf16[2,128,8,5,128]{4,1,3,2,0:T(8,128)(2,1)S(1)}, bf16[2,128,8,5,128]{4,1,3,2,0:T(8,128)(2,1)}, u32[]{:S(2)}) copy-start(bf16[2,128,8,5,128]{4,1,3,2,0:T(8,128)(2,1)} %get-tuple-element.214) | copy-start | bytes 7864324 | tf_op jit(solution)/shard_map/while
  272.5 108.5 %all-to-all-start.2 = ((bf16[128,128,256]{2,1,0:T(8,128)(2,1)}), bf16[128,128,256]{2,1,0:T(8,128)(2,1)}, u32[]{:S(2)}, u32[]{:S(2)}) async-start(bf16[128,128,256]{2,1,0:T(8,128)(2,1)} %bitcast.195), calls=%async_computation.2 | async-start | bytes 16777216 | tf_op jit(solution)/shard_map/all_to_all | solution.py:96
  381.0 16.0 %copy-start.11 = (pred[128]{0:T(512)(128)(4,1)S(1)}, pred[128]{0:T(512)(128)(4,1)}, u32[]{:S(2)}) copy-start(pred[128]{0:T(512)(128)(4,1)} %copy-done.10) | copy-start | bytes 388
  397.1 11.4 %copy-start.13 = (s32[128]{0:T(128)S(1)}, s32[128]{0:T(128)}, u32[]{:S(2)}) copy-start(s32[128]{0:T(128)} %copy-done.12) | copy-start | bytes 1540
where the time goes:
time: 443 us; the launch traced here: 435 us
  waiting for transfers between devices  157 us (35%)
  local copies, waits for them, and re-layouts  130 us (29%)
  other arithmetic  75.8 us (17%)
  matrix products  42.5 us (10%)
  starting transfers between devices  27.6 us (6%)
    all_to_all x1, waiting for transfers between devices, shards(): lax.all_to_all(returning.astype(jnp.bfloat16), ('ctx', 'bulk'), split_axi...  94.9 us
    all_to_all x1, waiting for transfers between devices, shards(): lax.all_to_all(outgoing, ('ctx', 'bulk'), split_axis=0, concat_axis=0, ti...  58.6 us
    unnamed x29, local copies, waits for them, and re-layouts  52.5 us
    scatter-add x1, other arithmetic, shards(): total = own_part.at[jnp.maximum(incoming, 0)].add(received_flat)  24.5 us
    dot_general x2, matrix products, block_grads(): jnp.einsum('qhgd,hjkd->hgqjk', grads, value_set, preferred_element_type=j...  12.9 us
    scatter x1, local copies, waits for them, and re-layouts, shards(): jnp.zeros((count_peers, BLK * 2 * HD), jnp.float32).at[target]  12.9 us
    slice x2, local copies, waits for them, and re-layouts, shards(): remote = partials[:, :, 1:].reshape(per_device, BLK * 2 * HD)  12.9 us
    dot_general x2, matrix products, block_grads(): jnp.einsum('hgqjk,qhgd->hjkd', probs, grads, preferred_element_type=jnp.f...  12.7 us
  transfers between devices with their start and end apart: 3, of which 3 were waited for; matrix products, arithmetic and copies ran while one was open for 11% of the time, Pallas kernels for 0%

commit v1 on v0

v1 whole, which is shorter than its diff:
```python
import functools

import jax
import jax.numpy as jnp
from jax import lax
from jax.experimental import pallas as pl
from jax.experimental.pallas import tpu as pltpu
from jax.sharding import PartitionSpec as P

HD = 128
KVH = 8
GROUP = 5
BLK = 128
TOPK = 3
LANES = 128
CHUNKS = (32, 32, 32, 32)
LOG2E = 1.4426950408889634
SCALE = HD ** (-0.5)
MESH = pl.DeviceIdType.MESH
NT = (((1,), (1,)), ((), ()))
TN = (((0,), (0,)), ((), ()))
NN = (((1,), (0,)), ((), ()))


def dot(a, b, dims):
    return lax.dot_general(a, b, dims, preferred_element_type=jnp.float32)


def kernel(n, bulk, local_blocks, *refs):
    nc = len(CHUNKS)
    starts = [sum(CHUNKS[:c]) for c in range(nc)]
    items = local_blocks * KVH
    rows_q = GROUP * BLK
    refs = list(refs)

    def take(count):
        out = refs[:count]
        del refs[:count]
        return out

    q_hbm, g_hbm, o_hbm, k_hbm, v_hbm, lse_ref, comb_v, comb_s, sel_s = take(9)
    gq_hbm, gk_hbm, gv_hbm = take(3)
    q_s, g_s, o_s, kv_s, dq_s, own_s, delta_s, part_s, run_s, gq_s, gk_s, gv_s = take(12)
    reqs, tab_v, tab_s = take(3)
    out_c = take(nc)
    inf_c = take(nc)
    inb_c = take(nc)
    load_sem, misc_sem, send_sem, req_send, req_recv, recv_sem = take(6)

    me = lax.axis_index("ctx") * bulk + lax.axis_index("bulk")

    def place(peer):
        return (peer // bulk, peer % bulk)

    barrier = pltpu.get_barrier_semaphore()

    def greet(step, _):
        peer = (me + step) % n
        pl.semaphore_signal(barrier, inc=1, device_id=place(peer), device_id_type=MESH)
        return _

    lax.fori_loop(1, n, greet, 0)

    def load_heads(index, _):
        b = index // (KVH * GROUP)
        i = index % (KVH * GROUP)
        src = (pl.ds(pl.multiple_of(b * BLK, BLK), BLK), pl.ds(pl.multiple_of(i * HD, HD), HD))
        at = pl.ds(pl.multiple_of((i % GROUP) * BLK, BLK), BLK)
        item = b * KVH + i // GROUP
        pltpu.make_async_copy(g_hbm.at[src], g_s.at[item, at], load_sem.at[0]).start()
        pltpu.make_async_copy(o_hbm.at[src], o_s.at[item, at], load_sem.at[1]).start()
        pltpu.make_async_copy(q_hbm.at[src], q_s.at[item, at], load_sem.at[2]).start()
        return _

    def load_kv(index, _):
        b = index // KVH
        h = index % KVH
        src = (pl.ds(pl.multiple_of(b * BLK, BLK), BLK), pl.ds(pl.multiple_of(h * HD, HD), HD))
        pltpu.make_async_copy(k_hbm.at[src], kv_s.at[index, pl.ds(0, BLK)], load_sem.at[3]).start()
        pltpu.make_async_copy(v_hbm.at[src], kv_s.at[index, pl.ds(BLK, BLK)], load_sem.at[3]).start()
        return _

    lax.fori_loop(0, items, load_kv, 0)
    lax.fori_loop(0, items * GROUP, load_heads, 0)
    pl.semaphore_wait(barrier, n - 1)

    def req_copy(peer, row):
        at = pl.ds(pl.multiple_of(row * 8, 8), 8)
        return pltpu.make_async_remote_copy(
            src_ref=comb_v,
            dst_ref=reqs.at[at],
            send_sem=req_send.at[peer],
            recv_sem=req_recv.at[row],
            device_id=place(peer),
            device_id_type=MESH,
        )

    def send_req(peer, _):
        req_copy(peer, me).start()
        return _

    lax.fori_loop(0, me, send_req, 0)

    pltpu.make_async_copy(g_s, g_s, load_sem.at[0]).wait()
    pltpu.make_async_copy(o_s, o_s, load_sem.at[1]).wait()
    lane = lax.broadcasted_iota(jnp.int32, (BLK, LANES), 1)
    row = lax.broadcasted_iota(jnp.int32, (BLK, LANES), 0)
    for b in range(local_blocks):

        def one_delta(i, acc):
            item = b * KVH + i // GROUP
            at = pl.ds(pl.multiple_of((i % GROUP) * BLK, BLK), BLK)
            prod = g_s[item, at, :].astype(jnp.float32) * o_s[item, at, :].astype(jnp.float32)
            return jnp.where(lane == i, jnp.sum(prod, axis=1, keepdims=True), acc)

        acc = lax.fori_loop(0, KVH * GROUP, one_delta, jnp.zeros((BLK, LANES), jnp.float32))
        delta_s[b] = acc.T

    def wait_req(peer, _):
        req_copy(peer, peer).wait_recv()
        return _

    lax.fori_loop(me + 1, n, wait_req, 0)

    codes = reqs[pl.ds(0, n, 8), :]
    lane_n = lax.broadcasted_iota(jnp.int32, (n, LANES), 1)
    row_n = lax.broadcasted_iota(jnp.int32, (n, LANES), 0)
    code_col = jnp.sum(jnp.where((lane_n == me) & (row_n > me), codes, 0), axis=1, keepdims=True)
    code_col = jnp.where(row_n[:, :1] > me, code_col, -1)
    item_col = jnp.where(code_col >= 0, code_col % items, items)
    item_full = jnp.broadcast_to(item_col, (n, LANES))
    key_full = item_full * LANES + row_n
    diag = row_n == lane_n
    item_row = jnp.sum(jnp.where(diag, item_full, 0), axis=0, keepdims=True)
    key_row = jnp.sum(jnp.where(diag, key_full, 0), axis=0, keepdims=True)
    key_row = jnp.where(lane_n[:1] < n, key_row, LANES * LANES)
    rank_col = jnp.sum(jnp.where(key_row < key_full, 1, 0), axis=1, keepdims=True)
    order_row = jnp.sum(jnp.where(rank_col == lane_n, row_n, 0), axis=0, keepdims=True)
    upto_row = jnp.sum(jnp.where(item_full <= lane_n, 1, 0), axis=0, keepdims=True)
    below_row = jnp.sum(jnp.where(item_full < lane_n, 1, 0), axis=0, keepdims=True)
    sorted_row = jnp.sum(jnp.where(rank_col == lane_n, item_full, 0), axis=0, keepdims=True)
    tab_v[0:1, :] = jnp.minimum(item_row, items - 1)
    tab_v[1:2, :] = order_row
    tab_v[2:3, :] = jnp.maximum(upto_row - 1, 0)
    tab_v[3:4, :] = jnp.where(upto_row > below_row, 1, 0)
    tab_v[4:5, :] = sorted_row
    tab_copy = pltpu.make_async_copy(tab_v, tab_s, misc_sem.at[0])
    tab_copy.start()
    pltpu.make_async_copy(kv_s, kv_s, load_sem.at[3]).wait()
    tab_copy.wait()

    def data_copy(c, peer, source, box):
        return pltpu.make_async_remote_copy(
            src_ref=out_c[c].at[peer],
            dst_ref=box[c].at[source],
            send_sem=send_sem.at[c],
            recv_sem=recv_sem.at[c, source],
            device_id=place(peer),
            device_id_type=MESH,
        )

    stride = 37 if n == 128 else 1

    def stage_keys(c):
        size, at = CHUNKS[c], starts[c]

        def one(peer, _):
            want = tab_s[0, peer]
            out_c[c][peer, 0:size, :] = kv_s[want, at : at + size, :]
            out_c[c][peer, size : 2 * size, :] = kv_s[want, BLK + at : BLK + at + size, :]
            return _

        lax.fori_loop(me + 1, n, one, 0)

    def send_keys(c):
        def one(step, _):
            peer = (me + step * stride) % n

            @pl.when(peer > me)
            def go():
                data_copy(c, peer, me, inf_c).start()

            return _

        lax.fori_loop(1, n, one, 0)

    def stage_grads(c):
        def one(peer, _):
            slot = jnp.maximum(comb_s[peer], 0) // items
            out_c[c][peer] = part_s[slot, 0 : 2 * CHUNKS[c], :]
            return _

        lax.fori_loop(0, me, one, 0)

    def send_grads(c):
        def one(step, _):
            peer = (me + n - (step * stride) % n) % n

            @pl.when(peer < me)
            def go():
                data_copy(c, peer, me, inb_c).start()

            return _

        lax.fori_loop(1, n, one, 0)

    def wait_keys(c):
        def one(peer, _):
            data_copy(c, peer, peer, inf_c).wait_recv()
            return _

        lax.fori_loop(0, me, one, 0)

    def wait_grads(c):
        def one(peer, _):
            data_copy(c, peer, peer, inb_c).wait_recv()
            return _

        lax.fori_loop(me + 1, n, one, 0)

    def rows_of(item, box):
        b, h = item // KVH, item % KVH
        return jnp.concatenate([box[b, pl.ds(h * GROUP + g, 1), :] for g in range(GROUP)], axis=1)

    def attend(item, key_set, value_set, mask):
        queries, grads = q_s[item], g_s[item]
        scores = dot(key_set, queries, NT)
        probs32 = jnp.exp2(scores * (SCALE * LOG2E) - rows_of(item, lse_ref) * LOG2E)
        if mask is not None:
            probs32 = jnp.where(mask, probs32, 0.0)
        dprobs = dot(value_set, grads, NT)
        dscores = (probs32 * (dprobs - rows_of(item, delta_s))).astype(jnp.bfloat16)
        value_part = dot(probs32.astype(jnp.bfloat16), grads, NN)
        key_part = dot(dscores, queries, NN)
        return key_part, value_part, dot(key_set, dscores, TN)

    def own_block(item, _):
        key_at = lax.broadcasted_iota(jnp.int32, (BLK, rows_q), 0)
        query_at = lax.broadcasted_iota(jnp.int32, (BLK, rows_q), 1) % BLK
        key_part, value_part, query_part = attend(
            item, kv_s[item, 0:BLK, :], kv_s[item, BLK : 2 * BLK, :], key_at <= query_at
        )
        own_s[item, 0:BLK, :] = key_part
        own_s[item, BLK : 2 * BLK, :] = value_part
        dq_s[item] = query_part
        return _

    def chunk_grads(c):
        size = CHUNKS[c]

        def one(item, _):
            sets = []
            for s in range(TOPK):
                chosen = sel_s[item * TOPK + s]
                owner = jnp.where(chosen >= 0, chosen // local_blocks, n)
                sets.append(inf_c[c][owner])
            key_set = jnp.concatenate([x[:size] for x in sets], axis=0)
            value_set = jnp.concatenate([x[size:] for x in sets], axis=0)
            key_part, value_part, query_part = attend(item, key_set, value_set, None)
            for s in range(TOPK):
                at = slice(s * size, (s + 1) * size)
                part_s[item * TOPK + s, 0:size, :] = key_part[at].astype(jnp.bfloat16)
                part_s[item * TOPK + s, size : 2 * size, :] = value_part[at].astype(jnp.bfloat16)
            dq_s[item] += query_part
            return _

        lax.fori_loop(0, items, one, 0)

    def fold(c):
        size, at = CHUNKS[c], starts[c]

        def scan(k, acc):
            source = tab_s[1, k]
            fresh = (tab_s[4, k] != tab_s[4, jnp.maximum(k - 1, 0)]) | (k == 0)
            keep = jnp.where(fresh, 0.0, 1.0)
            acc = acc * keep + inb_c[c][source].astype(jnp.float32)
            run_s[k, 0 : 2 * size, :] = acc
            return acc

        lax.fori_loop(0, n - 1 - me, scan, jnp.zeros((2 * size, HD), jnp.float32))

        def finish(item, _):
            last = jnp.where(tab_s[3, item] > 0, tab_s[2, item], n)
            total = run_s[last, 0 : 2 * size, :]
            b, h = item // KVH, item % KVH
            rows = pl.ds(pl.multiple_of(b * BLK + at, 16), size)
            cols = pl.ds(pl.multiple_of(h * HD, HD), HD)
            key_sum = own_s[item, at : at + size, :] + total[:size]
            value_sum = own_s[item, BLK + at : BLK + at + size, :] + total[size:]
            gk_s[rows, cols] = (key_sum * SCALE).astype(jnp.bfloat16)
            gv_s[rows, cols] = value_sum.astype(jnp.bfloat16)
            return _

        lax.fori_loop(0, items, finish, 0)

    for c in range(nc):
        inf_c[c][n] = jnp.zeros((2 * CHUNKS[c], HD), jnp.bfloat16)
    run_s[n] = jnp.zeros(run_s.shape[1:], jnp.float32)

    stage_keys(0)
    if nc > 1:
        stage_keys(1)
    send_keys(0)
    if nc > 1:
        send_keys(1)
    for c in range(2, nc):
        stage_keys(c)
    pltpu.make_async_copy(q_s, q_s, load_sem.at[2]).wait()
    lax.fori_loop(0, items, own_block, 0)

    for c in range(nc):
        wait_keys(c)
        chunk_grads(c)
        stage_grads(c)
        send_grads(c)
        if c + 2 < nc:
            send_keys(c + 2)

    def finish_query(index, _):
        b = index // (KVH * GROUP)
        i = index % (KVH * GROUP)
        item = b * KVH + i // GROUP
        cols = pl.ds(pl.multiple_of((i % GROUP) * BLK, BLK), BLK)
        rows = pl.ds(pl.multiple_of(b * BLK, BLK), BLK)
        part = dq_s[item, :, cols].T * SCALE
        gq_s[rows, pl.ds(pl.multiple_of(i * HD, HD), HD)] = part.astype(jnp.bfloat16)
        return _

    lax.fori_loop(0, items * GROUP, finish_query, 0)
    out_q = pltpu.make_async_copy(gq_s, gq_hbm, misc_sem.at[1])
    out_q.start()

    for c in range(nc):
        wait_grads(c)
        fold(c)
    out_k = pltpu.make_async_copy(gk_s, gk_hbm, misc_sem.at[2])
    out_v = pltpu.make_async_copy(gv_s, gv_hbm, misc_sem.at[3])
    out_k.start()
    out_v.start()

    def wait_req_sent(peer, _):
        req_copy(peer, me).wait_send()
        return _

    lax.fori_loop(0, me, wait_req_sent, 0)
    for c in range(nc):
        sent = out_c[c].at[pl.ds(0, n - 1)]
        pltpu.make_async_copy(sent, sent, send_sem.at[c]).wait()
    out_q.wait()
    out_k.wait()
    out_v.wait()


def shards(query, keys, values, output, grad_out, logsumexp, selected):
    bulk = lax.axis_size("bulk")
    n = lax.axis_size("ctx") * bulk
    tokens = query.shape[0]
    local_blocks = tokens // BLK
    items = local_blocks * KVH
    per_device = items * TOPK
    chosen = selected.reshape(per_device)
    slots = jnp.arange(per_device, dtype=jnp.int32)
    code = slots * items + chosen % local_blocks * KVH + slots // TOPK % KVH
    owners = jnp.where(chosen >= 0, chosen // local_blocks, -1)
    matches = owners[:, None] == jnp.arange(LANES, dtype=jnp.int32)[None, :]
    comb = jnp.max(jnp.where(matches, code[:, None], -1), axis=0)
    comb_tile = jnp.broadcast_to(comb[None, :], (8, LANES))
    lse = jnp.transpose(logsumexp.reshape(local_blocks, BLK, KVH * GROUP), (0, 2, 1))
    bf16, f32, i32 = jnp.bfloat16, jnp.float32, jnp.int32
    nc = len(CHUNKS)
    widest = max(CHUNKS)
    any_spec = pl.BlockSpec(memory_space=pl.ANY)
    vmem = pl.BlockSpec(memory_space=pltpu.VMEM)
    smem = pl.BlockSpec(memory_space=pltpu.SMEM)
    scratch = [
        pltpu.VMEM((items, GROUP * BLK, HD), bf16),
        pltpu.VMEM((items, GROUP * BLK, HD), bf16),
        pltpu.VMEM((items, GROUP * BLK, HD), bf16),
        pltpu.VMEM((items, 2 * BLK, HD), bf16),
        pltpu.VMEM((items, HD, GROUP * BLK), f32),
        pltpu.VMEM((items, 2 * BLK, HD), f32),
        pltpu.VMEM((local_blocks, LANES, BLK), f32),
        pltpu.VMEM((per_device, 2 * widest, HD), bf16),
        pltpu.VMEM((n + 1, 2 * widest, HD), f32),
        pltpu.VMEM(query.shape, bf16),
        pltpu.VMEM(keys.shape, bf16),
        pltpu.VMEM(values.shape, bf16),
        pltpu.VMEM((8 * n, LANES), i32),
        pltpu.VMEM((8, LANES), i32),
        pltpu.SMEM((8, LANES), i32),
        *[pltpu.VMEM((n, 2 * size, HD), bf16) for size in CHUNKS],
        *[pltpu.VMEM((n + 1, 2 * size, HD), bf16) for size in CHUNKS],
        *[pltpu.VMEM((n, 2 * size, HD), bf16) for size in CHUNKS],
        pltpu.SemaphoreType.DMA((4,)),
        pltpu.SemaphoreType.DMA((4,)),
        pltpu.SemaphoreType.DMA((nc,)),
        pltpu.SemaphoreType.DMA((n,)),
        pltpu.SemaphoreType.DMA((n,)),
        pltpu.SemaphoreType.DMA((nc, n)),
    ]
    return pl.pallas_call(
        functools.partial(kernel, n, bulk, local_blocks),
        out_shape=(
            jax.ShapeDtypeStruct(query.shape, bf16),
            jax.ShapeDtypeStruct(keys.shape, bf16),
            jax.ShapeDtypeStruct(values.shape, bf16),
        ),
        in_specs=[any_spec] * 5 + [vmem, vmem, smem, smem],
        out_specs=(any_spec,) * 3,
        scratch_shapes=scratch,
        compiler_params=pltpu.CompilerParams(
            collective_id=0, has_side_effects=True, vmem_limit_bytes=63_000_000
        ),
        name="block_sparse_backward",
    )(query, grad_out, output, keys, values, lse, comb_tile, comb, chosen)


def solution(mesh):
    rows = P(("ctx", "bulk"), None)
    in_specs = (rows,) * 6 + (P(("ctx", "bulk"), None, None),)
    return jax.shard_map(
        shards, mesh=mesh, in_specs=in_specs, out_specs=(rows,) * 3, check_vma=False
    )
```

time: 443 us -> 210 us (0.47)
  the two profiles are of different devices: /device:TPU:15 before, /device:TPU:33 now
where the time goes in v1:
time: 210 us
  Pallas kernels  202 us (96%)
  local copies, waits for them, and re-layouts  7.18 us (3%)
    pallas_call x1, Pallas kernels, shards(): pl.pallas_call(functools.partial(kernel, n, bulk, local_blocks), out_shap...  202 us
    unnamed x14, local copies, waits for them, and re-layouts  5.87 us

profile of v1, /device:TPU:33, one launch (start us, length us, event | category | flops | bytes accessed | tf_op | source)
XLA Modules:
  0.0 209.8 jit_solution(16698965651627286188)
XLA Ops:
  0.6 0.0 copy-start
  0.6 0.8 copy.14
  1.4 0.1 reshape.97.refs_8_
  1.5 0.0 copy-start.3
  1.5 0.1 select_reduce_fusion.refs_7_
  1.6 0.0 copy-start.4
  1.6 0.6 broadcast_in_dim.25.refs_6_
  2.2 0.0 copy-done
  2.2 0.6 bitcast_bitcast_fusion.refs_5_
  2.9 0.0 copy-done.3
  2.9 0.0 copy-done.4
  2.9 201.8 %block_sparse_backward.1 = (bf16[256,5120]{1,0:T(8,128)(2,1)}, bf16[256,1024]{1,0:T(8,128)(2,1)}, bf16[256,1024]{1,0:T(8,128)(2,1)}) custom-call(bf16[256,5120]{1,0:T(8,128)(2,1)} %refs_0_.1, bf16[256,5120]{1,0:T(8,128)(2,1)} %refs_1_.1, bf16[256,5120]{1,0:T(8,128)(2,1)} %refs_2_.1, bf16[256,1024]{1,0:T(8,128)(2,1)} %refs_3_.1, bf16[256,1024]{1,0:T(8,128)(2,1)} %refs_4_.1, ...), custom_call_target="tpu_custom_call" | custom-call | tf_op jit(solution)/shard_map/block_sparse_backward/pallas_call | solution.py:401
  204.7 0.0 copy-start.2
  204.7 0.0 copy-start.1
  204.7 3.5 %copy.20 = bf16[256,5120]{1,0:T(8,128)(2,1)} copy(bf16[256,5120]{1,0:T(8,128)(2,1)} %get-tuple-element.8) | data formatting | bytes 5242880
  208.2 0.0 copy-done.2
  208.2 0.8 copy.21
  209.0 0.0 copy-done.1
  209.0 0.8 copy.22
  (1 shorter events, 0.0 us)
Async XLA Ops:
  0.6 1.6 copy-start
  1.5 1.4 copy-start.3
  1.6 1.2 copy-start.4
  204.7 3.5 %copy-start.2 = (bf16[256,1024]{1,0:T(8,128)(2,1)S(1)}, bf16[256,1024]{1,0:T(8,128)(2,1)}, u32[]{:S(2)}) copy-start(bf16[256,1024]{1,0:T(8,128)(2,1)} %get-tuple-element.9) | copy-start | bytes 1572868
  204.7 4.3 %copy-start.1 = (bf16[256,1024]{1,0:T(8,128)(2,1)S(1)}, bf16[256,1024]{1,0:T(8,128)(2,1)}, u32[]{:S(2)}) copy-start(bf16[256,1024]{1,0:T(8,128)(2,1)} %get-tuple-element.10) | copy-start | bytes 1572868

commit v2 on v1

--- a/solution.py
+++ b/solution.py
@@ -13,7 +13,9 @@
 BLK = 128
 TOPK = 3
 LANES = 128
-CHUNKS = (32, 32, 32, 32)
+CHUNKS = (16,) * 8
+AHEAD = 2
+STRIDE = 37
 LOG2E = 1.4426950408889634
 SCALE = HD ** (-0.5)
 MESH = pl.DeviceIdType.MESH
@@ -38,10 +40,10 @@
         del refs[:count]
         return out
 
-    q_hbm, g_hbm, o_hbm, k_hbm, v_hbm, lse_ref, comb_v, comb_s, sel_s = take(9)
+    q_hbm, g_hbm, o_hbm, k_hbm, v_hbm, lse_ref, comb_s, sel_s = take(8)
     gq_hbm, gk_hbm, gv_hbm = take(3)
     q_s, g_s, o_s, kv_s, dq_s, own_s, delta_s, part_s, run_s, gq_s, gk_s, gv_s = take(12)
-    reqs, tab_v, tab_s = take(3)
+    reqs_s, reqs_v, tab_v, tab_s = take(4)
     out_c = take(nc)
     inf_c = take(nc)
     inb_c = take(nc)
@@ -85,10 +87,9 @@
     pl.semaphore_wait(barrier, n - 1)
 
     def req_copy(peer, row):
-        at = pl.ds(pl.multiple_of(row * 8, 8), 8)
         return pltpu.make_async_remote_copy(
-            src_ref=comb_v,
-            dst_ref=reqs.at[at],
+            src_ref=comb_s,
+            dst_ref=reqs_s.at[pl.ds(row, 1)],
             send_sem=req_send.at[peer],
             recv_sem=req_recv.at[row],
             device_id=place(peer),
@@ -122,32 +123,7 @@
 
     lax.fori_loop(me + 1, n, wait_req, 0)
 
-    codes = reqs[pl.ds(0, n, 8), :]
-    lane_n = lax.broadcasted_iota(jnp.int32, (n, LANES), 1)
-    row_n = lax.broadcasted_iota(jnp.int32, (n, LANES), 0)
-    code_col = jnp.sum(jnp.where((lane_n == me) & (row_n > me), codes, 0), axis=1, keepdims=True)
-    code_col = jnp.where(row_n[:, :1] > me, code_col, -1)
-    item_col = jnp.where(code_col >= 0, code_col % items, items)
-    item_full = jnp.broadcast_to(item_col, (n, LANES))
-    key_full = item_full * LANES + row_n
-    diag = row_n == lane_n
-    item_row = jnp.sum(jnp.where(diag, item_full, 0), axis=0, keepdims=True)
-    key_row = jnp.sum(jnp.where(diag, key_full, 0), axis=0, keepdims=True)
-    key_row = jnp.where(lane_n[:1] < n, key_row, LANES * LANES)
-    rank_col = jnp.sum(jnp.where(key_row < key_full, 1, 0), axis=1, keepdims=True)
-    order_row = jnp.sum(jnp.where(rank_col == lane_n, row_n, 0), axis=0, keepdims=True)
-    upto_row = jnp.sum(jnp.where(item_full <= lane_n, 1, 0), axis=0, keepdims=True)
-    below_row = jnp.sum(jnp.where(item_full < lane_n, 1, 0), axis=0, keepdims=True)
-    sorted_row = jnp.sum(jnp.where(rank_col == lane_n, item_full, 0), axis=0, keepdims=True)
-    tab_v[0:1, :] = jnp.minimum(item_row, items - 1)
-    tab_v[1:2, :] = order_row
-    tab_v[2:3, :] = jnp.maximum(upto_row - 1, 0)
-    tab_v[3:4, :] = jnp.where(upto_row > below_row, 1, 0)
-    tab_v[4:5, :] = sorted_row
-    tab_copy = pltpu.make_async_copy(tab_v, tab_s, misc_sem.at[0])
-    tab_copy.start()
     pltpu.make_async_copy(kv_s, kv_s, load_sem.at[3]).wait()
-    tab_copy.wait()
 
     def data_copy(c, peer, source, box):
         return pltpu.make_async_remote_copy(
@@ -159,26 +135,33 @@
             device_id_type=MESH,
         )
 
-    stride = 37 if n == 128 else 1
+    stride = STRIDE if n == 128 else 1
 
     def stage_keys(c):
         size, at = CHUNKS[c], starts[c]
 
         def one(peer, _):
-            want = tab_s[0, peer]
+            want = lax.rem(jnp.maximum(reqs_s[peer, me], 0), items)
             out_c[c][peer, 0:size, :] = kv_s[want, at : at + size, :]
             out_c[c][peer, size : 2 * size, :] = kv_s[want, BLK + at : BLK + at + size, :]
             return _
 
         lax.fori_loop(me + 1, n, one, 0)
 
-    def send_keys(c):
+    def send(keys_c, grads_c):
         def one(step, _):
             peer = (me + step * stride) % n
-
-            @pl.when(peer > me)
-            def go():
-                data_copy(c, peer, me, inf_c).start()
+            if keys_c is not None:
+
+                @pl.when(peer > me)
+                def go_keys():
+                    data_copy(keys_c, peer, me, inf_c).start()
+
+            if grads_c is not None:
+
+                @pl.when(peer < me)
+                def go_grads():
+                    data_copy(grads_c, peer, me, inb_c).start()
 
             return _
 
@@ -186,23 +169,11 @@
 
     def stage_grads(c):
         def one(peer, _):
-            slot = jnp.maximum(comb_s[peer], 0) // items
+            slot = lax.div(jnp.maximum(comb_s[0, peer], 0), items)
             out_c[c][peer] = part_s[slot, 0 : 2 * CHUNKS[c], :]
             return _
 
         lax.fori_loop(0, me, one, 0)
-
-    def send_grads(c):
-        def one(step, _):
-            peer = (me + n - (step * stride) % n) % n
-
-            @pl.when(peer < me)
-            def go():
-                data_copy(c, peer, me, inb_c).start()
-
-            return _
-
-        lax.fori_loop(1, n, one, 0)
 
     def wait_keys(c):
         def one(peer, _):
@@ -293,18 +264,39 @@
 
         lax.fori_loop(0, items, finish, 0)
 
+    for c in range(AHEAD):
+        stage_keys(c)
+        send(c, None)
+    req_vector = pltpu.make_async_copy(reqs_s, reqs_v, misc_sem.at[4])
+    req_vector.start()
     for c in range(nc):
         inf_c[c][n] = jnp.zeros((2 * CHUNKS[c], HD), jnp.bfloat16)
     run_s[n] = jnp.zeros(run_s.shape[1:], jnp.float32)
-
-    stage_keys(0)
-    if nc > 1:
-        stage_keys(1)
-    send_keys(0)
-    if nc > 1:
-        send_keys(1)
-    for c in range(2, nc):
+    for c in range(AHEAD, nc):
         stage_keys(c)
+    req_vector.wait()
+    lane_n = lax.broadcasted_iota(jnp.int32, (n, LANES), 1)
+    row_n = lax.broadcasted_iota(jnp.int32, (n, LANES), 0)
+    code_col = jnp.sum(jnp.where((lane_n == me) & (row_n > me), reqs_v[...], 0), axis=1, keepdims=True)
+    code_col = jnp.where(row_n[:, :1] > me, code_col, -1)
+    item_col = jnp.where(code_col >= 0, code_col % items, items)
+    item_full = jnp.broadcast_to(item_col, (n, LANES))
+    key_full = item_full * LANES + row_n
+    diag = row_n == lane_n
+    key_row = jnp.sum(jnp.where(diag, key_full, 0), axis=0, keepdims=True)
+    key_row = jnp.where(lane_n[:1] < n, key_row, LANES * LANES)
+    rank_col = jnp.sum(jnp.where(key_row < key_full, 1, 0), axis=1, keepdims=True)
+    order_row = jnp.sum(jnp.where(rank_col == lane_n, row_n, 0), axis=0, keepdims=True)
+    upto_row = jnp.sum(jnp.where(item_full <= lane_n, 1, 0), axis=0, keepdims=True)
+    below_row = jnp.sum(jnp.where(item_full < lane_n, 1, 0), axis=0, keepdims=True)
+    sorted_row = jnp.sum(jnp.where(rank_col == lane_n, item_full, 0), axis=0, keepdims=True)
+    tab_v[1:2, :] = order_row
+    tab_v[2:3, :] = jnp.maximum(upto_row - 1, 0)
+    tab_v[3:4, :] = jnp.where(upto_row > below_row, 1, 0)
+    tab_v[4:5, :] = sorted_row
+    tab_copy = pltpu.make_async_copy(tab_v, tab_s, misc_sem.at[0])
+    tab_copy.start()
+
     pltpu.make_async_copy(q_s, q_s, load_sem.at[2]).wait()
     lax.fori_loop(0, items, own_block, 0)
 
@@ -312,9 +304,8 @@
         wait_keys(c)
         chunk_grads(c)
         stage_grads(c)
-        send_grads(c)
-        if c + 2 < nc:
-            send_keys(c + 2)
+        send(c + AHEAD if c + AHEAD < nc else None, c)
+    tab_copy.wait()
 
     def finish_query(index, _):
         b = index // (KVH * GROUP)
@@ -364,7 +355,6 @@
     owners = jnp.where(chosen >= 0, chosen // local_blocks, -1)
     matches = owners[:, None] == jnp.arange(LANES, dtype=jnp.int32)[None, :]
     comb = jnp.max(jnp.where(matches, code[:, None], -1), axis=0)
-    comb_tile = jnp.broadcast_to(comb[None, :], (8, LANES))
     lse = jnp.transpose(logsumexp.reshape(local_blocks, BLK, KVH * GROUP), (0, 2, 1))
     bf16, f32, i32 = jnp.bfloat16, jnp.float32, jnp.int32
     nc = len(CHUNKS)
@@ -385,14 +375,15 @@
         pltpu.VMEM(query.shape, bf16),
         pltpu.VMEM(keys.shape, bf16),
         pltpu.VMEM(values.shape, bf16),
-        pltpu.VMEM((8 * n, LANES), i32),
+        pltpu.SMEM((n, LANES), i32),
+        pltpu.VMEM((n, LANES), i32),
         pltpu.VMEM((8, LANES), i32),
         pltpu.SMEM((8, LANES), i32),
         *[pltpu.VMEM((n, 2 * size, HD), bf16) for size in CHUNKS],
         *[pltpu.VMEM((n + 1, 2 * size, HD), bf16) for size in CHUNKS],
         *[pltpu.VMEM((n, 2 * size, HD), bf16) for size in CHUNKS],
         pltpu.SemaphoreType.DMA((4,)),
-        pltpu.SemaphoreType.DMA((4,)),
+        pltpu.SemaphoreType.DMA((5,)),
         pltpu.SemaphoreType.DMA((nc,)),
         pltpu.SemaphoreType.DMA((n,)),
         pltpu.SemaphoreType.DMA((n,)),
@@ -405,14 +396,14 @@
             jax.ShapeDtypeStruct(keys.shape, bf16),
             jax.ShapeDtypeStruct(values.shape, bf16),
         ),
-        in_specs=[any_spec] * 5 + [vmem, vmem, smem, smem],
+        in_specs=[any_spec] * 5 + [vmem, smem, smem],
         out_specs=(any_spec,) * 3,
         scratch_shapes=scratch,
         compiler_params=pltpu.CompilerParams(
             collective_id=0, has_side_effects=True, vmem_limit_bytes=63_000_000
         ),
         name="block_sparse_backward",
-    )(query, grad_out, output, keys, values, lse, comb_tile, comb, chosen)
+    )(query, grad_out, output, keys, values, lse, comb[None, :], chosen)
 
 
 def solution(mesh):

time: 210 us -> 182 us (0.87)
  Pallas kernels: 202 us -> 174 us
    pallas_call x1, Pallas kernels: 202 us -> 174 us  [shards(): pl.pallas_call(functools.partial(kernel, n, bulk, local_blocks), out_shap...]
    unnamed x14 -> x12, local copies, waits for them, and re-layouts: 5.87 us -> 5.87 us
where the time goes in v2:
time: 182 us
  Pallas kernels  174 us (96%)
  local copies, waits for them, and re-layouts  6.58 us (4%)
    pallas_call x1, Pallas kernels, shards(): pl.pallas_call(functools.partial(kernel, n, bulk, local_blocks), out_shap...  174 us
    unnamed x12, local copies, waits for them, and re-layouts  5.87 us

profile of v2, /device:TPU:33, one launch (start us, length us, event | category | flops | bytes accessed | tf_op | source)
XLA Modules:
  0.0 181.8 jit_solution(16629664950346107485)
XLA Ops:
  0.6 0.0 copy-start
  0.6 0.8 copy.14
  1.4 0.1 reshape.96.refs_7_
  1.5 0.0 copy-start.3
  1.5 0.6 select_reduce_fusion
  2.2 0.0 copy-done
  2.2 0.6 bitcast_bitcast_fusion.refs_5_
  2.8 0.0 copy-done.3
  2.8 173.9 %block_sparse_backward.1 = (bf16[256,5120]{1,0:T(8,128)(2,1)}, bf16[256,1024]{1,0:T(8,128)(2,1)}, bf16[256,1024]{1,0:T(8,128)(2,1)}) custom-call(bf16[256,5120]{1,0:T(8,128)(2,1)} %refs_0_.1, bf16[256,5120]{1,0:T(8,128)(2,1)} %refs_1_.1, bf16[256,5120]{1,0:T(8,128)(2,1)} %refs_2_.1, bf16[256,1024]{1,0:T(8,128)(2,1)} %refs_3_.1, bf16[256,1024]{1,0:T(8,128)(2,1)} %refs_4_.1, ...), custom_call_target="tpu_custom_call" | custom-call | tf_op jit(solution)/shard_map/block_sparse_backward/pallas_call | solution.py:392
  176.7 0.0 copy-start.2
  176.7 0.0 copy-start.1
  176.7 3.5 %copy.20 = bf16[256,5120]{1,0:T(8,128)(2,1)} copy(bf16[256,5120]{1,0:T(8,128)(2,1)} %get-tuple-element.8) | data formatting | bytes 5242880
  180.2 0.0 copy-done.2
  180.2 0.8 copy.21
  181.0 0.0 copy-done.1
  181.0 0.8 copy.22
  (1 shorter events, 0.0 us)
Async XLA Ops:
  0.6 1.5 copy-start
  1.5 1.3 copy-start.3
  176.7 3.5 %copy-start.2 = (bf16[256,1024]{1,0:T(8,128)(2,1)S(1)}, bf16[256,1024]{1,0:T(8,128)(2,1)}, u32[]{:S(2)}) copy-start(bf16[256,1024]{1,0:T(8,128)(2,1)} %get-tuple-element.9) | copy-start | bytes 1572868
  176.7 4.3 %copy-start.1 = (bf16[256,1024]{1,0:T(8,128)(2,1)S(1)}, bf16[256,1024]{1,0:T(8,128)(2,1)}, u32[]{:S(2)}) copy-start(bf16[256,1024]{1,0:T(8,128)(2,1)} %get-tuple-element.10) | copy-start | bytes 1572868

commit v3 on v2

--- a/solution.py
+++ b/solution.py
@@ -15,7 +15,8 @@
 LANES = 128
 CHUNKS = (16,) * 8
 AHEAD = 2
-STRIDE = 37
+STRIDE = 91
+UNROLL = 4
 LOG2E = 1.4426950408889634
 SCALE = HD ** (-0.5)
 MESH = pl.DeviceIdType.MESH
@@ -44,7 +45,8 @@
     gq_hbm, gk_hbm, gv_hbm = take(3)
     q_s, g_s, o_s, kv_s, dq_s, own_s, delta_s, part_s, run_s, gq_s, gk_s, gv_s = take(12)
     reqs_s, reqs_v, tab_v, tab_s = take(4)
-    out_c = take(nc)
+    outf_c = take(nc)
+    outb_c = take(nc)
     inf_c = take(nc)
     inb_c = take(nc)
     load_sem, misc_sem, send_sem, req_send, req_recv, recv_sem = take(6)
@@ -52,12 +54,12 @@
     me = lax.axis_index("ctx") * bulk + lax.axis_index("bulk")
 
     def place(peer):
-        return (peer // bulk, peer % bulk)
+        return (lax.div(peer, bulk), lax.rem(peer, bulk))
 
     barrier = pltpu.get_barrier_semaphore()
 
     def greet(step, _):
-        peer = (me + step) % n
+        peer = lax.rem(me + step, n)
         pl.semaphore_signal(barrier, inc=1, device_id=place(peer), device_id_type=MESH)
         return _
 
@@ -125,11 +127,11 @@
 
     pltpu.make_async_copy(kv_s, kv_s, load_sem.at[3]).wait()
 
-    def data_copy(c, peer, source, box):
+    def data_copy(c, peer, source, out, box, turn=0):
         return pltpu.make_async_remote_copy(
-            src_ref=out_c[c].at[peer],
+            src_ref=out[c].at[peer],
             dst_ref=box[c].at[source],
-            send_sem=send_sem.at[c],
+            send_sem=send_sem.at[turn % 2, peer],
             recv_sem=recv_sem.at[c, source],
             device_id=place(peer),
             device_id_type=MESH,
@@ -142,49 +144,67 @@
 
         def one(peer, _):
             want = lax.rem(jnp.maximum(reqs_s[peer, me], 0), items)
-            out_c[c][peer, 0:size, :] = kv_s[want, at : at + size, :]
-            out_c[c][peer, size : 2 * size, :] = kv_s[want, BLK + at : BLK + at + size, :]
-            return _
-
-        lax.fori_loop(me + 1, n, one, 0)
-
-    def send(keys_c, grads_c):
+            outf_c[c][peer, 0:size, :] = kv_s[want, at : at + size, :]
+            outf_c[c][peer, size : 2 * size, :] = kv_s[want, BLK + at : BLK + at + size, :]
+            return _
+
+        lax.fori_loop(0, n, one, 0, unroll=UNROLL)
+
+    def wait_sent(turn):
+        def keys_sent(peer, _):
+            data_copy(turn, peer, me, outf_c, inf_c, turn).wait_send()
+            return _
+
+        def grads_sent(peer, _):
+            data_copy(turn - AHEAD, peer, me, outb_c, inb_c, turn).wait_send()
+            return _
+
+        if 0 <= turn < nc:
+            lax.fori_loop(me + 1, n, keys_sent, 0)
+        if AHEAD <= turn:
+            lax.fori_loop(0, me, grads_sent, 0)
+
+    def send(turn):
+        keys_c = turn if turn < nc else None
+        grads_c = turn - AHEAD if turn >= AHEAD else None
+        wait_sent(turn - 2)
+
         def one(step, _):
-            peer = (me + step * stride) % n
+            peer = lax.rem(me + step * stride, n)
             if keys_c is not None:
 
                 @pl.when(peer > me)
                 def go_keys():
-                    data_copy(keys_c, peer, me, inf_c).start()
+                    data_copy(keys_c, peer, me, outf_c, inf_c, turn).start()
 
             if grads_c is not None:
 
                 @pl.when(peer < me)
                 def go_grads():
-                    data_copy(grads_c, peer, me, inb_c).start()
-
-            return _
-
-        lax.fori_loop(1, n, one, 0)
+                    data_copy(grads_c, peer, me, outb_c, inb_c, turn).start()
+
+            return _
+
+        lax.fori_loop(0, n, one, 0, unroll=UNROLL)
 
     def stage_grads(c):
         def one(peer, _):
             slot = lax.div(jnp.maximum(comb_s[0, peer], 0), items)
-            out_c[c][peer] = part_s[slot, 0 : 2 * CHUNKS[c], :]
-            return _
-
-        lax.fori_loop(0, me, one, 0)
+            outb_c[c][peer] = part_s[slot, 0 : 2 * CHUNKS[c], :]
+            return _
+
+        lax.fori_loop(0, n, one, 0, unroll=UNROLL)
 
     def wait_keys(c):
         def one(peer, _):
-            data_copy(c, peer, peer, inf_c).wait_recv()
+            data_copy(c, peer, peer, outf_c, inf_c).wait_recv()
             return _
 
         lax.fori_loop(0, me, one, 0)
 
     def wait_grads(c):
         def one(peer, _):
-            data_copy(c, peer, peer, inb_c).wait_recv()
+            data_copy(c, peer, peer, outb_c, inb_c).wait_recv()
             return _
 
         lax.fori_loop(me + 1, n, one, 0)
@@ -242,13 +262,11 @@
 
         def scan(k, acc):
             source = tab_s[1, k]
-            fresh = (tab_s[4, k] != tab_s[4, jnp.maximum(k - 1, 0)]) | (k == 0)
-            keep = jnp.where(fresh, 0.0, 1.0)
-            acc = acc * keep + inb_c[c][source].astype(jnp.float32)
+            acc = jnp.where(tab_s[4, k] > 0, 0.0, acc) + inb_c[c][source].astype(jnp.float32)
             run_s[k, 0 : 2 * size, :] = acc
             return acc
 
-        lax.fori_loop(0, n - 1 - me, scan, jnp.zeros((2 * size, HD), jnp.float32))
+        lax.fori_loop(0, n, scan, jnp.zeros((2 * size, HD), jnp.float32), unroll=UNROLL)
 
         def finish(item, _):
             last = jnp.where(tab_s[3, item] > 0, tab_s[2, item], n)
@@ -262,11 +280,11 @@
             gv_s[rows, cols] = value_sum.astype(jnp.bfloat16)
             return _
 
-        lax.fori_loop(0, items, finish, 0)
+        lax.fori_loop(0, items, finish, 0, unroll=UNROLL)
 
     for c in range(AHEAD):
         stage_keys(c)
-        send(c, None)
+        send(c)
     req_vector = pltpu.make_async_copy(reqs_s, reqs_v, misc_sem.at[4])
     req_vector.start()
     for c in range(nc):
@@ -283,17 +301,21 @@
     item_full = jnp.broadcast_to(item_col, (n, LANES))
     key_full = item_full * LANES + row_n
     diag = row_n == lane_n
+    item_row = jnp.sum(jnp.where(diag, item_full, 0), axis=0, keepdims=True)
+    item_row = jnp.where(lane_n[:1] < n, item_row, items)
     key_row = jnp.sum(jnp.where(diag, key_full, 0), axis=0, keepdims=True)
     key_row = jnp.where(lane_n[:1] < n, key_row, LANES * LANES)
     rank_col = jnp.sum(jnp.where(key_row < key_full, 1, 0), axis=1, keepdims=True)
     order_row = jnp.sum(jnp.where(rank_col == lane_n, row_n, 0), axis=0, keepdims=True)
     upto_row = jnp.sum(jnp.where(item_full <= lane_n, 1, 0), axis=0, keepdims=True)
     below_row = jnp.sum(jnp.where(item_full < lane_n, 1, 0), axis=0, keepdims=True)
-    sorted_row = jnp.sum(jnp.where(rank_col == lane_n, item_full, 0), axis=0, keepdims=True)
+    lead_col = jnp.sum(jnp.where(item_row < item_full, 1, 0), axis=1, keepdims=True)
+    lead_col = jnp.where(lead_col == rank_col, 1, 0)
+    fresh_row = jnp.sum(jnp.where(rank_col == lane_n, lead_col, 0), axis=0, keepdims=True)
     tab_v[1:2, :] = order_row
     tab_v[2:3, :] = jnp.maximum(upto_row - 1, 0)
     tab_v[3:4, :] = jnp.where(upto_row > below_row, 1, 0)
-    tab_v[4:5, :] = sorted_row
+    tab_v[4:5, :] = fresh_row
     tab_copy = pltpu.make_async_copy(tab_v, tab_s, misc_sem.at[0])
     tab_copy.start()
 
@@ -304,7 +326,7 @@
         wait_keys(c)
         chunk_grads(c)
         stage_grads(c)
-        send(c + AHEAD if c + AHEAD < nc else None, c)
+        send(c + AHEAD)
     tab_copy.wait()
 
     def finish_query(index, _):
@@ -334,9 +356,8 @@
         return _
 
     lax.fori_loop(0, me, wait_req_sent, 0)
-    for c in range(nc):
-        sent = out_c[c].at[pl.ds(0, n - 1)]
-        pltpu.make_async_copy(sent, sent, send_sem.at[c]).wait()
+    wait_sent(nc + AHEAD - 2)
+    wait_sent(nc + AHEAD - 1)
     out_q.wait()
     out_k.wait()
     out_v.wait()
@@ -380,11 +401,12 @@
         pltpu.VMEM((8, LANES), i32),
         pltpu.SMEM((8, LANES), i32),
         *[pltpu.VMEM((n, 2 * size, HD), bf16) for size in CHUNKS],
+        *[pltpu.VMEM((n, 2 * size, HD), bf16) for size in CHUNKS],
         *[pltpu.VMEM((n + 1, 2 * size, HD), bf16) for size in CHUNKS],
         *[pltpu.VMEM((n, 2 * size, HD), bf16) for size in CHUNKS],
         pltpu.SemaphoreType.DMA((4,)),
         pltpu.SemaphoreType.DMA((5,)),
-        pltpu.SemaphoreType.DMA((nc,)),
+        pltpu.SemaphoreType.DMA((2, n)),
         pltpu.SemaphoreType.DMA((n,)),
         pltpu.SemaphoreType.DMA((n,)),
         pltpu.SemaphoreType.DMA((nc, n)),

time: 182 us -> 185 us (1.016)
  the two profiles are of different devices: /device:TPU:33 before, /device:TPU:72 now
where the time goes in v3:
time: 185 us
  Pallas kernels  177 us (96%)
  local copies, waits for them, and re-layouts  6.58 us (4%)
    pallas_call x1, Pallas kernels, shards(): pl.pallas_call(functools.partial(kernel, n, bulk, local_blocks), out_shap...  177 us
    unnamed x12, local copies, waits for them, and re-layouts  5.87 us

profile of v3, /device:TPU:72, one launch (start us, length us, event | category | flops | bytes accessed | tf_op | source)
XLA Modules:
  0.0 184.7 jit_solution(1117144388712309646)
XLA Ops:
  0.6 0.0 copy-start
  0.6 0.8 copy.14
  1.4 0.1 reshape.96.refs_7_
  1.5 0.0 copy-start.3
  1.5 0.6 select_reduce_fusion
  2.2 0.0 copy-done
  2.2 0.6 bitcast_bitcast_fusion.refs_5_
  2.8 0.0 copy-done.3
  2.8 176.8 %block_sparse_backward.1 = (bf16[256,5120]{1,0:T(8,128)(2,1)}, bf16[256,1024]{1,0:T(8,128)(2,1)}, bf16[256,1024]{1,0:T(8,128)(2,1)}) custom-call(bf16[256,5120]{1,0:T(8,128)(2,1)} %refs_0_.1, bf16[256,5120]{1,0:T(8,128)(2,1)} %refs_1_.1, bf16[256,5120]{1,0:T(8,128)(2,1)} %refs_2_.1, bf16[256,1024]{1,0:T(8,128)(2,1)} %refs_3_.1, bf16[256,1024]{1,0:T(8,128)(2,1)} %refs_4_.1, ...), custom_call_target="tpu_custom_call" | custom-call | tf_op jit(solution)/shard_map/block_sparse_backward/pallas_call | solution.py:414
  179.6 0.0 copy-start.2
  179.6 0.0 copy-start.1
  179.6 3.5 %copy.20 = bf16[256,5120]{1,0:T(8,128)(2,1)} copy(bf16[256,5120]{1,0:T(8,128)(2,1)} %get-tuple-element.8) | data formatting | bytes 5242880
  183.1 0.0 copy-done.2
  183.1 0.8 copy.21
  183.9 0.0 copy-done.1
  183.9 0.8 copy.22
  (1 shorter events, 0.0 us)
Async XLA Ops:
  0.6 1.5 copy-start
  1.5 1.3 copy-start.3
  179.6 3.5 %copy-start.2 = (bf16[256,1024]{1,0:T(8,128)(2,1)S(1)}, bf16[256,1024]{1,0:T(8,128)(2,1)}, u32[]{:S(2)}) copy-start(bf16[256,1024]{1,0:T(8,128)(2,1)} %get-tuple-element.9) | copy-start | bytes 1572868
  179.6 4.3 %copy-start.1 = (bf16[256,1024]{1,0:T(8,128)(2,1)S(1)}, bf16[256,1024]{1,0:T(8,128)(2,1)}, u32[]{:S(2)}) copy-start(bf16[256,1024]{1,0:T(8,128)(2,1)} %get-tuple-element.10) | copy-start | bytes 1572868

commit v4 on v2

--- a/solution.py
+++ b/solution.py
@@ -16,6 +16,7 @@
 CHUNKS = (16,) * 8
 AHEAD = 2
 STRIDE = 37
+UNROLL = 4
 LOG2E = 1.4426950408889634
 SCALE = HD ** (-0.5)
 MESH = pl.DeviceIdType.MESH
@@ -242,13 +243,11 @@
 
         def scan(k, acc):
             source = tab_s[1, k]
-            fresh = (tab_s[4, k] != tab_s[4, jnp.maximum(k - 1, 0)]) | (k == 0)
-            keep = jnp.where(fresh, 0.0, 1.0)
-            acc = acc * keep + inb_c[c][source].astype(jnp.float32)
+            acc = jnp.where(tab_s[4, k] > 0, 0.0, acc) + inb_c[c][source].astype(jnp.float32)
             run_s[k, 0 : 2 * size, :] = acc
             return acc
 
-        lax.fori_loop(0, n - 1 - me, scan, jnp.zeros((2 * size, HD), jnp.float32))
+        lax.fori_loop(0, n, scan, jnp.zeros((2 * size, HD), jnp.float32), unroll=UNROLL)
 
         def finish(item, _):
             last = jnp.where(tab_s[3, item] > 0, tab_s[2, item], n)
@@ -262,7 +261,7 @@
             gv_s[rows, cols] = value_sum.astype(jnp.bfloat16)
             return _
 
-        lax.fori_loop(0, items, finish, 0)
+        lax.fori_loop(0, items, finish, 0, unroll=UNROLL)
 
     for c in range(AHEAD):
         stage_keys(c)
@@ -283,17 +282,21 @@
     item_full = jnp.broadcast_to(item_col, (n, LANES))
     key_full = item_full * LANES + row_n
     diag = row_n == lane_n
+    item_row = jnp.sum(jnp.where(diag, item_full, 0), axis=0, keepdims=True)
+    item_row = jnp.where(lane_n[:1] < n, item_row, items)
     key_row = jnp.sum(jnp.where(diag, key_full, 0), axis=0, keepdims=True)
     key_row = jnp.where(lane_n[:1] < n, key_row, LANES * LANES)
     rank_col = jnp.sum(jnp.where(key_row < key_full, 1, 0), axis=1, keepdims=True)
     order_row = jnp.sum(jnp.where(rank_col == lane_n, row_n, 0), axis=0, keepdims=True)
     upto_row = jnp.sum(jnp.where(item_full <= lane_n, 1, 0), axis=0, keepdims=True)
     below_row = jnp.sum(jnp.where(item_full < lane_n, 1, 0), axis=0, keepdims=True)
-    sorted_row = jnp.sum(jnp.where(rank_col == lane_n, item_full, 0), axis=0, keepdims=True)
+    lead_col = jnp.sum(jnp.where(item_row < item_full, 1, 0), axis=1, keepdims=True)
+    lead_col = jnp.where(lead_col == rank_col, 1, 0)
+    fresh_row = jnp.sum(jnp.where(rank_col == lane_n, lead_col, 0), axis=0, keepdims=True)
     tab_v[1:2, :] = order_row
     tab_v[2:3, :] = jnp.maximum(upto_row - 1, 0)
     tab_v[3:4, :] = jnp.where(upto_row > below_row, 1, 0)
-    tab_v[4:5, :] = sorted_row
+    tab_v[4:5, :] = fresh_row
     tab_copy = pltpu.make_async_copy(tab_v, tab_s, misc_sem.at[0])
     tab_copy.start()
 

time: 182 us -> 179 us (0.984); the launches traced: 182 us -> 177 us
  Pallas kernels: 174 us -> 169 us
    pallas_call x1, Pallas kernels: 174 us -> 169 us  [shards(): pl.pallas_call(functools.partial(kernel, n, bulk, local_blocks), out_shap...]
where the time goes in v4:
time: 179 us; the launch traced here: 177 us
  Pallas kernels  169 us (94%)
  local copies, waits for them, and re-layouts  6.58 us (4%)
    pallas_call x1, Pallas kernels, shards(): pl.pallas_call(functools.partial(kernel, n, bulk, local_blocks), out_shap...  169 us
    unnamed x12, local copies, waits for them, and re-layouts  5.87 us

profile of v4, /device:TPU:33, one launch (start us, length us, event | category | flops | bytes accessed | tf_op | source)
XLA Modules:
  0.0 176.8 jit_solution(10088486238869301682)
XLA Ops:
  0.6 0.0 copy-start
  0.6 0.8 copy.14
  1.4 0.1 reshape.96.refs_7_
  1.5 0.0 copy-start.3
  1.5 0.6 select_reduce_fusion
  2.2 0.0 copy-done
  2.2 0.6 bitcast_bitcast_fusion.refs_5_
  2.8 0.0 copy-done.3
  2.8 169.0 %block_sparse_backward.1 = (bf16[256,5120]{1,0:T(8,128)(2,1)}, bf16[256,1024]{1,0:T(8,128)(2,1)}, bf16[256,1024]{1,0:T(8,128)(2,1)}) custom-call(bf16[256,5120]{1,0:T(8,128)(2,1)} %refs_0_.1, bf16[256,5120]{1,0:T(8,128)(2,1)} %refs_1_.1, bf16[256,5120]{1,0:T(8,128)(2,1)} %refs_2_.1, bf16[256,1024]{1,0:T(8,128)(2,1)} %refs_3_.1, bf16[256,1024]{1,0:T(8,128)(2,1)} %refs_4_.1, ...), custom_call_target="tpu_custom_call" | custom-call | tf_op jit(solution)/shard_map/block_sparse_backward/pallas_call | solution.py:395
  171.7 0.0 copy-start.2
  171.8 0.0 copy-start.1
  171.8 3.5 %copy.20 = bf16[256,5120]{1,0:T(8,128)(2,1)} copy(bf16[256,5120]{1,0:T(8,128)(2,1)} %get-tuple-element.8) | data formatting | bytes 5242880
  175.3 0.0 copy-done.2
  175.3 0.8 copy.21
  176.1 0.0 copy-done.1
  176.1 0.8 copy.22
  (1 shorter events, 0.0 us)
Async XLA Ops:
  0.6 1.5 copy-start
  1.5 1.3 copy-start.3
  171.7 3.5 %copy-start.2 = (bf16[256,1024]{1,0:T(8,128)(2,1)S(1)}, bf16[256,1024]{1,0:T(8,128)(2,1)}, u32[]{:S(2)}) copy-start(bf16[256,1024]{1,0:T(8,128)(2,1)} %get-tuple-element.9) | copy-start | bytes 1572868
  171.8 4.3 %copy-start.1 = (bf16[256,1024]{1,0:T(8,128)(2,1)S(1)}, bf16[256,1024]{1,0:T(8,128)(2,1)}, u32[]{:S(2)}) copy-start(bf16[256,1024]{1,0:T(8,128)(2,1)} %get-tuple-element.10) | copy-start | bytes 1572868
